TPU v7x, 32 devices: a whole 2x2x4 slice. The times are simulated.
32 devices in a mesh: gz: 8 (over z, x), gy: 4 (over y, core).
Axes of the slice: x: 2, y: 2, z: 4, core: 2. Of those that a mesh axis runs over, the one named last changes fastest.
Arguments:
- source_first: float32 [64, 32, 16, 128], P('gz', 'gy'), may hold values from -6 to 6
- source_second: float32 [32, 16, 16, 128], P('gz', 'gy'), may hold values from -6 to 6
- source_third: float32 [16, 8, 16, 128], P('gz', 'gy'), may hold values from -6 to 6
- source_fourth: float32 [8, 4, 16, 128], P('gz', 'gy'), may hold values from -6 to 6
- guess_first: float32 [64, 32, 16, 128], P('gz', 'gy'), may hold values from -6 to 6
- guess_second: float32 [32, 16, 16, 128], P('gz', 'gy'), may hold values from -6 to 6
- guess_third: float32 [16, 8, 16, 128], P('gz', 'gy'), may hold values from -6 to 6
- guess_fourth: float32 [8, 4, 16, 128], P('gz', 'gy'), may hold values from -6 to 6
- shift_first: float32 [64, 32, 128], P('gz', 'gy'), may hold values from 0.2 to 2
- shift_second: float32 [32, 16, 128], P('gz', 'gy'), may hold values from 0.2 to 2
- shift_third: float32 [16, 8, 128], P('gz', 'gy'), may hold values from 0.2 to 2
- shift_fourth: float32 [8, 4, 128], P('gz', 'gy'), may hold values from 0.2 to 2
- blocks_first: bfloat16 [64, 32, 2, 128, 128], P('gz', 'gy'), may hold values from -0.375 to 0.375
- blocks_second: bfloat16 [32, 16, 2, 128, 128], P('gz', 'gy'), may hold values from -0.375 to 0.375
- blocks_third: bfloat16 [16, 8, 2, 128, 128], P('gz', 'gy'), may hold values from -0.375 to 0.375
- links_first: int32 [64, 32, 2], P('gz', 'gy'), may hold values from 0 to 511, as said below
- links_second: int32 [32, 16, 2], P('gz', 'gy'), may hold values from 0 to 127, as said below
- links_third: int32 [16, 8, 2], P('gz', 'gy'), may hold values from 0 to 31, as said below
Outputs:
- smooth_first: float32 [64, 32, 16, 128], P('gz', 'gy')
- smooth_second: float32 [32, 16, 16, 128], P('gz', 'gy')
- smooth_third: float32 [16, 8, 16, 128], P('gz', 'gy')
- smooth_fourth: float32 [8, 4, 16, 128], P('gz', 'gy')
Inputs may be any that keep to these rules, and one draw needn't show every extreme that they name: `links_first`: entry k of fine cell (i, j) names coarse column x * 16 + y with x within one of i // 2 and y within one of j // 2, both periodic on the coarse grid. `links_second`: entry k of cell (i, j) names coarse column x * 8 + y with x within one of i // 2 and y within one of j // 2, both periodic on the coarse grid. `links_third`: entry k of cell (i, j) names coarse column x * 4 + y with x within one of i // 2 and y within one of j // 2, both periodic on the coarse grid.
All inputs are finite; a program needn't handle non-finite values.
Results may differ from a plain program's by a relative error of at most 0.0005.
Values may be sent and summed in bfloat16 or wider, within the bound.
A program may use at most 256 MiB of HBM per device.

v0:
```python
from functools import partial

import jax
import jax.numpy as jnp
from jax import lax
from jax.sharding import PartitionSpec as P

DEGREE = 3


upper_edge = 14.0
lower_edge = upper_edge / 8.0


def padded(x, sides, width):
    for axis, dim in sides:
        peers, length = (lax.axis_size(axis), x.shape[dim])
        up = [(i, (i + 1) % peers) for i in range(peers)]
        down = [(j, i) for i, j in up]
        last = lax.slice_in_dim(x, length - width, length, axis=dim)
        initial = lax.slice_in_dim(x, 0, width, axis=dim)
        before = lax.ppermute(last, axis, up)
        after = lax.ppermute(initial, axis, down)
        x = jnp.concatenate([before, x, after], axis=dim)
    return x


def chebyshev(source, initial, operator):
    centre = (upper_edge + lower_edge) / 2.0
    half_width = (upper_edge - lower_edge) / 2.0
    ratio_edge = centre / half_width
    factor = 1.0 / ratio_edge
    residual = source - operator(initial)
    direction = residual / centre
    result = initial
    for sweep_index in range(DEGREE):
        result = result + direction
        if sweep_index + 1 < DEGREE:
            residual = residual - operator(direction)
            factor_next = 1.0 / (2.0 * ratio_edge - factor)
            direction = factor_next * factor * direction + 2.0 * factor_next / half_width * residual
            factor = factor_next
    return result


def line_sum(vector):
    return jnp.roll(vector, 1, 3) + jnp.roll(vector, -1, 3)


def spread_apply(vector, diagonal):
    extended = padded(vector, (("gz", 0), ("gy", 1)), 1)
    beside = extended[2:, 1:-1] + extended[:-2, 1:-1] + extended[1:-1, 2:] + extended[1:-1, :-2]
    beside = beside + line_sum(vector)
    return (6.0 + diagonal[:, :, None, :]) * vector - beside


def slab_apply(vector, diagonal):
    extended = padded(vector, (("gz", 0),), 1)
    beside = extended[2:] + extended[:-2] + jnp.roll(vector, 1, 1) + jnp.roll(vector, -1, 1)
    beside = beside + line_sum(vector)
    return (6.0 + diagonal[:, :, None, :]) * vector - beside


def pack_level(source, initial, diagonal):
    return jnp.concatenate([source, initial, diagonal[:, :, None, :]], axis=2)


def level_smooth(source, initial, diagonal):
    return chebyshev(source, initial, partial(spread_apply, diagonal=diagonal))


def gathered_smooth(source, initial, diagonal):
    copies = source.shape[2]
    gathered = lax.all_gather(pack_level(source, initial, diagonal), "gy", axis=1, tiled=True)
    return chebyshev(
        gathered[:, :, :copies],
        gathered[:, :, copies : 2 * copies],
        partial(slab_apply, diagonal=gathered[:, :, 2 * copies]),
    )


def own_rows(gathered):
    row_count = gathered.shape[1] // lax.axis_size("gy")
    return lax.dynamic_slice_in_dim(gathered, lax.axis_index("gy") * row_count, row_count, 1)


def prolong_local(extended, link_ids, blocks, anchor_row, anchor_col, full_rows, full_cols):
    coarse_row = link_ids // full_cols
    coarse_col = link_ids % full_cols
    local_row = (coarse_row - anchor_row + 1) % full_rows
    local_col = (coarse_col - anchor_col + 1) % full_cols
    flat_index = local_row * extended.shape[1] + local_col
    picked_lines = extended.reshape((-1,) + extended.shape[2:])[flat_index]
    return jnp.einsum("abkrj,abkij->abri", picked_lines, blocks, preferred_element_type=jnp.float32)


def spread_prolong(coarse, link_ids, blocks):
    narrow = coarse.astype(jnp.bfloat16)
    extended = padded(narrow, (("gz", 0), ("gy", 1)), 1)
    return prolong_local(
        extended,
        link_ids,
        blocks,
        lax.axis_index("gz") * coarse.shape[0],
        lax.axis_index("gy") * coarse.shape[1],
        coarse.shape[0] * lax.axis_size("gz"),
        coarse.shape[1] * lax.axis_size("gy"),
    )


def slab_prolong(gathered, link_ids, blocks):
    narrow = gathered.astype(jnp.bfloat16)
    extended = padded(narrow, (("gz", 0),), 1)
    extended = jnp.concatenate([extended[:, -1:], extended, extended[:, :1]], axis=1)
    return prolong_local(
        extended,
        link_ids,
        blocks,
        lax.axis_index("gz") * gathered.shape[0],
        0,
        gathered.shape[0] * lax.axis_size("gz"),
        gathered.shape[1],
    )


def shards(
    source_first,
    source_second,
    source_third,
    source_fourth,
    guess_first,
    guess_second,
    guess_third,
    guess_fourth,
    shift_first,
    shift_second,
    shift_third,
    shift_fourth,
    blocks_first,
    blocks_second,
    blocks_third,
    links_first,
    links_second,
    links_third,
):
    fourth_whole = gathered_smooth(source_fourth, guess_fourth, shift_fourth)
    smooth_fourth = own_rows(fourth_whole)
    start_third = guess_third + slab_prolong(fourth_whole, links_third, blocks_third)
    third_whole = gathered_smooth(source_third, start_third, shift_third)
    smooth_third = own_rows(third_whole)
    start_second = guess_second + slab_prolong(third_whole, links_second, blocks_second)
    smooth_second = level_smooth(source_second, start_second, shift_second)
    start_first = guess_first + spread_prolong(smooth_second, links_first, blocks_first)
    smooth_first = level_smooth(source_first, start_first, shift_first)
    return (smooth_first, smooth_second, smooth_third, smooth_fourth)


def solution(mesh):
    in_specs = (
        P("gz", "gy", None, None),
        P("gz", "gy", None, None),
        P("gz", "gy", None, None),
        P("gz", "gy", None, None),
        P("gz", "gy", None, None),
        P("gz", "gy", None, None),
        P("gz", "gy", None, None),
        P("gz", "gy", None, None),
        P("gz", "gy", None),
        P("gz", "gy", None),
        P("gz", "gy", None),
        P("gz", "gy", None),
        P("gz", "gy", None, None, None),
        P("gz", "gy", None, None, None),
        P("gz", "gy", None, None, None),
        P("gz", "gy", None),
        P("gz", "gy", None),
        P("gz", "gy", None),
    )
    out_specs = (
        P("gz", "gy", None, None),
        P("gz", "gy", None, None),
        P("gz", "gy", None, None),
        P("gz", "gy", None, None),
    )
    return jax.shard_map(shards, mesh=mesh, in_specs=in_specs, out_specs=out_specs, check_vma=False)
```

profile of v0, /device:TPU:0, one launch (start us, length us, event | category | flops | bytes accessed | tf_op | source)
XLA Modules:
  0.0 166.0 jit_solution(16387655743293812934)
XLA Ops:
  0.6 0.8 pad_maximum_fusion.85
  1.5 6.2 %all_gather.6 = f32[1,4,33,128]{3,0,2,1:T(1,128)S(1)} all-gather(f32[1,1,33,128]{3,0,2,1:T(1,128)S(1)} %pad_maximum_fusion.85), channel_id=1, replica_groups=mesh['gz'=8,'gy'=4] {'gy'}, dimensions={1}, use_global_device_ids=true | all-gather | bytes 84480 | tf_op jit(solution)/shard_map/all_gather | solution.py:74
  7.7 2.0 %collective-permute-start.1 = (f32[1,4,16,128]{3,2,1,0:T(8,128)S(1)}, f32[1,4,16,128]{3,2,1,0:T(8,128)S(1)}, u32[]{:S(2)}, u32[]{:S(2)}) collective-permute-start(f32[1,4,16,128]{3,2,1,0:T(8,128)S(1)} %bitcast.49), channel_id=1, source_target_pairs={{0,4},{4,8},{8,12},{12,16},{16,20},{20,24},{24,28},{28,0},{1,5},{5... | collective-permute-start | bytes 98312 | tf_op jit(solution)/shard_map/ppermute | solution.py:22
  9.7 3.1 %collective-permute-start = (f32[1,4,16,128]{3,2,1,0:T(8,128)S(1)}, f32[1,4,16,128]{3,2,1,0:T(8,128)S(1)}, u32[]{:S(2)}, u32[]{:S(2)}) collective-permute-start(f32[1,4,16,128]{3,2,1,0:T(8,128)S(1)} %bitcast.50), channel_id=1, source_target_pairs={{4,0},{8,4},{12,8},{16,12},{20,16},{24,20},{28,24},{0,28},{5,1},{9... | collective-permute-start | bytes 98312 | tf_op jit(solution)/shard_map/ppermute | solution.py:23
  13.1 0.7 compare_select_fusion.10
  13.9 0.7 broadcast_multiply_fusion.5
  14.6 0.8 broadcast_multiply_fusion.3
  15.4 0.7 compare_select_fusion.5
  16.1 0.8 compare_select_fusion
  17.3 4.7 %collective-permute-start.2 = (f32[1,4,16,128]{3,2,1,0:T(8,128)S(1)}, f32[1,4,16,128]{3,2,1,0:T(8,128)S(1)}, u32[]{:S(2)}, u32[]{:S(2)}) collective-permute-start(f32[1,4,16,128]{3,2,1,0:T(8,128)S(1)} %get-tuple-element.28), channel_id=1, source_target_pairs={{4,0},{8,4},{12,8},{16,12},{20,16},{24,20},{28,24},{0,28},{5,1},{9... | collective-permute-start | bytes 98312 | tf_op jit(solution)/shard_map/ppermute | solution.py:23
  22.1 1.7 %collective-permute-done.3 = f32[1,4,16,128]{3,2,1,0:T(8,128)S(1)} collective-permute-done((f32[1,4,16,128]{3,2,1,0:T(8,128)S(1)}, f32[1,4,16,128]{3,2,1,0:T(8,128)S(1)}, u32[]{:S(2)}, u32[]{:S(2)}) %collective-permute-start.3) | collective-permute-done | bytes 32800 | tf_op jit(solution)/shard_map/ppermute | solution.py:22
  24.0 4.8 %collective-permute-start.4 = (f32[1,4,16,128]{3,2,1,0:T(8,128)S(1)}, f32[1,4,16,128]{3,2,1,0:T(8,128)S(1)}, u32[]{:S(2)}, u32[]{:S(2)}) collective-permute-start(f32[1,4,16,128]{3,2,1,0:T(8,128)S(1)} %get-tuple-element.26), channel_id=1, source_target_pairs={{4,0},{8,4},{12,8},{16,12},{20,16},{24,20},{28,24},{0,28},{5,1},{9... | collective-permute-start | bytes 98312 | tf_op jit(solution)/shard_map/ppermute | solution.py:23
  29.0 1.7 %collective-permute-done.5 = f32[1,4,16,128]{3,2,1,0:T(8,128)S(1)} collective-permute-done((f32[1,4,16,128]{3,2,1,0:T(8,128)S(1)}, f32[1,4,16,128]{3,2,1,0:T(8,128)S(1)}, u32[]{:S(2)}, u32[]{:S(2)}) %collective-permute-start.5) | collective-permute-done | bytes 32800 | tf_op jit(solution)/shard_map/ppermute | solution.py:22
  30.8 4.8 %collective-permute-start.7 = (bf16[1,4,16,128]{3,2,1,0:T(8,128)(2,1)S(1)}, bf16[1,4,16,128]{3,2,1,0:T(8,128)(2,1)S(1)}, u32[]{:S(2)}, u32[]{:S(2)}) collective-permute-start(bf16[1,4,16,128]{3,2,1,0:T(8,128)(2,1)S(1)} %get-tuple-element.24), channel_id=1, source_target_pairs={{4,0},{8,4},{12,8},{16,12},{20,16},{24,20},{28,24},{0,28},{5,1},{9... | collective-permute-start | bytes 49160 | tf_op jit(solution)/shard_map/ppermute | solution.py:23
  35.9 1.2 collective-permute-done.7
  37.0 5.0 %collective-permute-done.6 = bf16[1,4,16,128]{3,2,1,0:T(8,128)(2,1)S(1)} collective-permute-done((bf16[1,4,16,128]{3,2,1,0:T(8,128)(2,1)S(1)}, bf16[1,4,16,128]{3,2,1,0:T(8,128)(2,1)S(1)}, u32[]{:S(2)}, u32[]{:S(2)}) %collective-permute-start.6) | collective-permute-done | bytes 16416 | tf_op jit(solution)/shard_map/ppermute | solution.py:22
  42.6 1.1 fusion.2
  43.7 0.8 pad_maximum_fusion.68
  44.5 6.3 %all_gather.7 = f32[2,8,33,128]{3,2,1,0:T(8,128)S(1)} all-gather(f32[2,2,33,128]{3,2,1,0:T(8,128)S(1)} %pad_maximum_fusion.68), channel_id=1, replica_groups=mesh['gz'=8,'gy'=4] {'gy'}, dimensions={1}, use_global_device_ids=true | all-gather | bytes 337920 | tf_op jit(solution)/shard_map/all_gather | solution.py:74
  51.1 2.0 %collective-permute-start.9 = (f32[1,8,16,128]{3,2,1,0:T(8,128)S(1)}, f32[1,8,16,128]{3,2,1,0:T(8,128)S(1)}, u32[]{:S(2)}, u32[]{:S(2)}) collective-permute-start(f32[1,8,16,128]{3,2,1,0:T(8,128)S(1)} %get-tuple-element.55), channel_id=1, source_target_pairs={{0,4},{4,8},{8,12},{12,16},{16,20},{20,24},{24,28},{28,0},{1,5},{5... | collective-permute-start | bytes 196616 | tf_op jit(solution)/shard_map/ppermute | solution.py:22
  53.1 2.3 %collective-permute-done.8 = f32[1,8,16,128]{3,2,1,0:T(8,128)S(1)} collective-permute-done((f32[1,8,16,128]{3,2,1,0:T(8,128)S(1)}, f32[1,8,16,128]{3,2,1,0:T(8,128)S(1)}, u32[]{:S(2)}, u32[]{:S(2)}) %collective-permute-start.8) | collective-permute-done | bytes 65568 | tf_op jit(solution)/shard_map/ppermute | solution.py:23
  55.4 2.8 %collective-permute-done.9 = f32[1,8,16,128]{3,2,1,0:T(8,128)S(1)} collective-permute-done((f32[1,8,16,128]{3,2,1,0:T(8,128)S(1)}, f32[1,8,16,128]{3,2,1,0:T(8,128)S(1)}, u32[]{:S(2)}, u32[]{:S(2)}) %collective-permute-start.9) | collective-permute-done | bytes 65568 | tf_op jit(solution)/shard_map/ppermute | solution.py:22
  58.9 1.8 %collective-permute-start.11 = (f32[1,8,16,128]{3,2,1,0:T(8,128)S(1)}, f32[1,8,16,128]{3,2,1,0:T(8,128)S(1)}, u32[]{:S(2)}, u32[]{:S(2)}) collective-permute-start(f32[1,8,16,128]{3,2,1,0:T(8,128)S(1)} %get-tuple-element.99), channel_id=1, source_target_pairs={{0,4},{4,8},{8,12},{12,16},{16,20},{20,24},{24,28},{28,0},{1,5},{5... | collective-permute-start | bytes 196616 | tf_op jit(solution)/shard_map/ppermute | solution.py:22
  60.7 2.2 %collective-permute-done.10 = f32[1,8,16,128]{3,2,1,0:T(8,128)S(1)} collective-permute-done((f32[1,8,16,128]{3,2,1,0:T(8,128)S(1)}, f32[1,8,16,128]{3,2,1,0:T(8,128)S(1)}, u32[]{:S(2)}, u32[]{:S(2)}) %collective-permute-start.10) | collective-permute-done | bytes 65568 | tf_op jit(solution)/shard_map/ppermute | solution.py:23
  62.9 2.9 %collective-permute-done.11 = f32[1,8,16,128]{3,2,1,0:T(8,128)S(1)} collective-permute-done((f32[1,8,16,128]{3,2,1,0:T(8,128)S(1)}, f32[1,8,16,128]{3,2,1,0:T(8,128)S(1)}, u32[]{:S(2)}, u32[]{:S(2)}) %collective-permute-start.11) | collective-permute-done | bytes 65568 | tf_op jit(solution)/shard_map/ppermute | solution.py:22
  66.3 2.0 %collective-permute-start.13 = (f32[1,8,16,128]{3,2,1,0:T(8,128)S(1)}, f32[1,8,16,128]{3,2,1,0:T(8,128)S(1)}, u32[]{:S(2)}, u32[]{:S(2)}) collective-permute-start(f32[1,8,16,128]{3,2,1,0:T(8,128)S(1)} %get-tuple-element.89), channel_id=1, source_target_pairs={{0,4},{4,8},{8,12},{12,16},{16,20},{20,24},{24,28},{28,0},{1,5},{5... | collective-permute-start | bytes 196616 | tf_op jit(solution)/shard_map/ppermute | solution.py:22
  68.3 2.9 %collective-permute-done.12 = f32[1,8,16,128]{3,2,1,0:T(8,128)S(1)} collective-permute-done((f32[1,8,16,128]{3,2,1,0:T(8,128)S(1)}, f32[1,8,16,128]{3,2,1,0:T(8,128)S(1)}, u32[]{:S(2)}, u32[]{:S(2)}) %collective-permute-start.12) | collective-permute-done | bytes 65568 | tf_op jit(solution)/shard_map/ppermute | solution.py:23
  71.3 2.1 %collective-permute-done.13 = f32[1,8,16,128]{3,2,1,0:T(8,128)S(1)} collective-permute-done((f32[1,8,16,128]{3,2,1,0:T(8,128)S(1)}, f32[1,8,16,128]{3,2,1,0:T(8,128)S(1)}, u32[]{:S(2)}, u32[]{:S(2)}) %collective-permute-start.13) | collective-permute-done | bytes 65568 | tf_op jit(solution)/shard_map/ppermute | solution.py:22
  73.6 4.7 %collective-permute-start.15 = (bf16[1,8,16,128]{3,2,1,0:T(8,128)(2,1)S(1)}, bf16[1,8,16,128]{3,2,1,0:T(8,128)(2,1)S(1)}, u32[]{:S(2)}, u32[]{:S(2)}) collective-permute-start(bf16[1,8,16,128]{3,2,1,0:T(8,128)(2,1)S(1)} %get-tuple-element.123), channel_id=1, source_target_pairs={{4,0},{8,4},{12,8},{16,12},{20,16},{24,20},{28,24},{0,28},{5,1},{9... | collective-permute-start | bytes 98312 | tf_op jit(solution)/shard_map/ppermute | solution.py:23
  78.3 1.9 %collective-permute-done.14 = bf16[1,8,16,128]{3,2,1,0:T(8,128)(2,1)S(1)} collective-permute-done((bf16[1,8,16,128]{3,2,1,0:T(8,128)(2,1)S(1)}, bf16[1,8,16,128]{3,2,1,0:T(8,128)(2,1)S(1)}, u32[]{:S(2)}, u32[]{:S(2)}) %collective-permute-start.14) | collective-permute-done | bytes 32800 | tf_op jit(solution)/shard_map/ppermute | solution.py:22
  81.3 4.9 %collective-permute-start.16 = (f32[1,4,16,128]{3,2,1,0:T(8,128)S(1)}, f32[1,4,16,128]{3,2,1,0:T(8,128)S(1)}, u32[]{:S(2)}, u32[]{:S(2)}) collective-permute-start(f32[1,4,16,128]{3,2,1,0:T(8,128)S(1)} %get-tuple-element.83), channel_id=1, source_target_pairs={{4,0},{8,4},{12,8},{16,12},{20,16},{24,20},{28,24},{0,28},{5,1},{9... | collective-permute-start | bytes 98312 | tf_op jit(solution)/shard_map/ppermute | solution.py:23
  86.2 1.7 %collective-permute-done.17 = f32[1,4,16,128]{3,2,1,0:T(8,128)S(1)} collective-permute-done((f32[1,4,16,128]{3,2,1,0:T(8,128)S(1)}, f32[1,4,16,128]{3,2,1,0:T(8,128)S(1)}, u32[]{:S(2)}, u32[]{:S(2)}) %collective-permute-start.17) | collective-permute-done | bytes 32800 | tf_op jit(solution)/shard_map/ppermute | solution.py:22
  88.7 1.1 collective-permute-done.18
  89.8 2.2 %collective-permute-done.19 = f32[6,1,16,128]{3,2,1,0:T(8,128)S(1)} collective-permute-done((f32[6,1,16,128]{3,2,1,0:T(8,128)S(1)}, f32[6,1,16,128]{3,2,1,0:T(8,128)S(1)}, u32[]{:S(2)}, u32[]{:S(2)}) %collective-permute-start.19) | collective-permute-done | bytes 49184 | tf_op jit(solution)/shard_map/ppermute | solution.py:22
  92.2 4.8 %collective-permute-start.20 = (f32[1,4,16,128]{3,2,1,0:T(8,128)S(1)}, f32[1,4,16,128]{3,2,1,0:T(8,128)S(1)}, u32[]{:S(2)}, u32[]{:S(2)}) collective-permute-start(f32[1,4,16,128]{3,2,1,0:T(8,128)S(1)} %get-tuple-element.77), channel_id=1, source_target_pairs={{4,0},{8,4},{12,8},{16,12},{20,16},{24,20},{28,24},{0,28},{5,1},{9... | collective-permute-start | bytes 98312 | tf_op jit(solution)/shard_map/ppermute | solution.py:23
  97.2 1.7 %collective-permute-done.21 = f32[1,4,16,128]{3,2,1,0:T(8,128)S(1)} collective-permute-done((f32[1,4,16,128]{3,2,1,0:T(8,128)S(1)}, f32[1,4,16,128]{3,2,1,0:T(8,128)S(1)}, u32[]{:S(2)}, u32[]{:S(2)}) %collective-permute-start.21) | collective-permute-done | bytes 32800 | tf_op jit(solution)/shard_map/ppermute | solution.py:22
  99.6 1.1 collective-permute-done.22
  100.7 1.8 %collective-permute-done.23 = f32[6,1,16,128]{3,2,1,0:T(8,128)S(1)} collective-permute-done((f32[6,1,16,128]{3,2,1,0:T(8,128)S(1)}, f32[6,1,16,128]{3,2,1,0:T(8,128)S(1)}, u32[]{:S(2)}, u32[]{:S(2)}) %collective-permute-start.23) | collective-permute-done | bytes 49184 | tf_op jit(solution)/shard_map/ppermute | solution.py:22
  102.8 4.8 %collective-permute-start.24 = (f32[1,4,16,128]{3,2,1,0:T(8,128)S(1)}, f32[1,4,16,128]{3,2,1,0:T(8,128)S(1)}, u32[]{:S(2)}, u32[]{:S(2)}) collective-permute-start(f32[1,4,16,128]{3,2,1,0:T(8,128)S(1)} %get-tuple-element.71), channel_id=1, source_target_pairs={{4,0},{8,4},{12,8},{16,12},{20,16},{24,20},{28,24},{0,28},{5,1},{9... | collective-permute-start | bytes 98312 | tf_op jit(solution)/shard_map/ppermute | solution.py:23
  107.7 1.7 %collective-permute-done.25 = f32[1,4,16,128]{3,2,1,0:T(8,128)S(1)} collective-permute-done((f32[1,4,16,128]{3,2,1,0:T(8,128)S(1)}, f32[1,4,16,128]{3,2,1,0:T(8,128)S(1)}, u32[]{:S(2)}, u32[]{:S(2)}) %collective-permute-start.25) | collective-permute-done | bytes 32800 | tf_op jit(solution)/shard_map/ppermute | solution.py:22
  110.1 1.1 collective-permute-done.26
  111.2 1.9 %collective-permute-done.27 = f32[6,1,16,128]{3,2,1,0:T(8,128)S(1)} collective-permute-done((f32[6,1,16,128]{3,2,1,0:T(8,128)S(1)}, f32[6,1,16,128]{3,2,1,0:T(8,128)S(1)}, u32[]{:S(2)}, u32[]{:S(2)}) %collective-permute-start.27) | collective-permute-done | bytes 49184 | tf_op jit(solution)/shard_map/ppermute | solution.py:22
  113.1 0.8 fusion.102
  113.9 4.8 %collective-permute-start.29 = (bf16[1,4,16,128]{3,2,1,0:T(8,128)(2,1)S(1)}, bf16[1,4,16,128]{3,2,1,0:T(8,128)(2,1)S(1)}, u32[]{:S(2)}, u32[]{:S(2)}) collective-permute-start(bf16[1,4,16,128]{3,2,1,0:T(8,128)(2,1)S(1)} %get-tuple-element.121), channel_id=1, source_target_pairs={{4,0},{8,4},{12,8},{16,12},{20,16},{24,20},{28,24},{0,28},{5,1},{9... | collective-permute-start | bytes 49160 | tf_op jit(solution)/shard_map/ppermute | solution.py:23
  119.3 1.1 collective-permute-done.28
  120.5 1.7 %collective-permute-start.31 = (bf16[6,1,16,128]{3,2,1,0:T(8,128)(2,1)S(1)}, bf16[6,1,16,128]{3,2,1,0:T(8,128)(2,1)S(1)}, u32[]{:S(2)}, u32[]{:S(2)}) collective-permute-start(bf16[6,1,16,128]{3,2,1,0:T(8,128)(2,1)S(1)} %get-tuple-element.109), channel_id=1, source_target_pairs={{1,0},{2,1},{3,2},{0,3},{5,4},{6,5},{7,6},{4,7},{9,8},{10,9},{11,1... | collective-permute-start | bytes 73736 | tf_op jit(solution)/shard_map/ppermute | solution.py:23
  122.3 0.6 constant_dynamic-slice_fusion.1
  122.9 0.9 collective-permute-done.30
  123.8 0.7 gather_fusion.2
  124.5 3.4 %fusion = f32[8,8,16,128]{3,2,1,0:T(8,128)S(1)} fusion(f32[8,8,16,128]{3,2,1,0:T(8,128)S(1)} %copy-done.2, bf16[8,8,2,16,128]{4,3,2,1,0:T(8,128)(2,1)S(1)} %bitcast.46, bf16[8,8,2,128,128]{4,3,2,1,0:T(8,128)(2,1)} %param.30), kind=kOutput, calls=%fused_computation.4 | convolution fusion | flops 67239936 | bytes 5767168 | tf_op jit(solution)/shard_map/abkrj,abkij->abri/dot_general | solution.py:94
  128.1 4.8 %collective-permute-start.32 = (f32[1,8,16,128]{3,2,1,0:T(8,128)S(1)}, f32[1,8,16,128]{3,2,1,0:T(8,128)S(1)}, u32[]{:S(2)}, u32[]{:S(2)}) collective-permute-start(f32[1,8,16,128]{3,2,1,0:T(8,128)S(1)} %get-tuple-element.49), channel_id=1, source_target_pairs={{4,0},{8,4},{12,8},{16,12},{20,16},{24,20},{28,24},{0,28},{5,1},{9... | collective-permute-start | bytes 196616 | tf_op jit(solution)/shard_map/ppermute | solution.py:23
  133.0 2.3 %collective-permute-done.33 = f32[1,8,16,128]{3,2,1,0:T(8,128)S(1)} collective-permute-done((f32[1,8,16,128]{3,2,1,0:T(8,128)S(1)}, f32[1,8,16,128]{3,2,1,0:T(8,128)S(1)}, u32[]{:S(2)}, u32[]{:S(2)}) %collective-permute-start.33) | collective-permute-done | bytes 65568 | tf_op jit(solution)/shard_map/ppermute | solution.py:22
  135.3 0.9 collective-permute-start.34
  136.4 2.2 %collective-permute-done.34 = f32[10,1,16,128]{3,2,1,0:T(8,128)S(1)} collective-permute-done((f32[10,1,16,128]{3,2,1,0:T(8,128)S(1)}, f32[10,1,16,128]{3,2,1,0:T(8,128)S(1)}, u32[]{:S(2)}, u32[]{:S(2)}) %collective-permute-start.34) | collective-permute-done | bytes 81952 | tf_op jit(solution)/shard_map/ppermute | solution.py:23
  138.6 2.0 %collective-permute-done.35 = f32[10,1,16,128]{3,2,1,0:T(8,128)S(1)} collective-permute-done((f32[10,1,16,128]{3,2,1,0:T(8,128)S(1)}, f32[10,1,16,128]{3,2,1,0:T(8,128)S(1)}, u32[]{:S(2)}, u32[]{:S(2)}) %collective-permute-start.35) | collective-permute-done | bytes 81952 | tf_op jit(solution)/shard_map/ppermute | solution.py:22
  141.1 5.0 %collective-permute-start.36 = (f32[1,8,16,128]{3,2,1,0:T(8,128)S(1)}, f32[1,8,16,128]{3,2,1,0:T(8,128)S(1)}, u32[]{:S(2)}, u32[]{:S(2)}) collective-permute-start(f32[1,8,16,128]{3,2,1,0:T(8,128)S(1)} %get-tuple-element.43), channel_id=1, source_target_pairs={{4,0},{8,4},{12,8},{16,12},{20,16},{24,20},{28,24},{0,28},{5,1},{9... | collective-permute-start | bytes 196616 | tf_op jit(solution)/shard_map/ppermute | solution.py:23
  146.3 2.0 %collective-permute-done.37 = f32[1,8,16,128]{3,2,1,0:T(8,128)S(1)} collective-permute-done((f32[1,8,16,128]{3,2,1,0:T(8,128)S(1)}, f32[1,8,16,128]{3,2,1,0:T(8,128)S(1)}, u32[]{:S(2)}, u32[]{:S(2)}) %collective-permute-start.37) | collective-permute-done | bytes 65568 | tf_op jit(solution)/shard_map/ppermute | solution.py:22
  149.1 1.7 %collective-permute-done.38 = f32[10,1,16,128]{3,2,1,0:T(8,128)S(1)} collective-permute-done((f32[10,1,16,128]{3,2,1,0:T(8,128)S(1)}, f32[10,1,16,128]{3,2,1,0:T(8,128)S(1)}, u32[]{:S(2)}, u32[]{:S(2)}) %collective-permute-start.38) | collective-permute-done | bytes 81952 | tf_op jit(solution)/shard_map/ppermute | solution.py:23
  150.8 1.8 %collective-permute-done.39 = f32[10,1,16,128]{3,2,1,0:T(8,128)S(1)} collective-permute-done((f32[10,1,16,128]{3,2,1,0:T(8,128)S(1)}, f32[10,1,16,128]{3,2,1,0:T(8,128)S(1)}, u32[]{:S(2)}, u32[]{:S(2)}) %collective-permute-start.39) | collective-permute-done | bytes 81952 | tf_op jit(solution)/shard_map/ppermute | solution.py:22
  153.2 4.8 %collective-permute-start.40 = (f32[1,8,16,128]{3,2,1,0:T(8,128)S(1)}, f32[1,8,16,128]{3,2,1,0:T(8,128)S(1)}, u32[]{:S(2)}, u32[]{:S(2)}) collective-permute-start(f32[1,8,16,128]{3,2,1,0:T(8,128)S(1)} %get-tuple-element.41), channel_id=1, source_target_pairs={{4,0},{8,4},{12,8},{16,12},{20,16},{24,20},{28,24},{0,28},{5,1},{9... | collective-permute-start | bytes 196616 | tf_op jit(solution)/shard_map/ppermute | solution.py:23
  158.2 2.0 %collective-permute-done.41 = f32[1,8,16,128]{3,2,1,0:T(8,128)S(1)} collective-permute-done((f32[1,8,16,128]{3,2,1,0:T(8,128)S(1)}, f32[1,8,16,128]{3,2,1,0:T(8,128)S(1)}, u32[]{:S(2)}, u32[]{:S(2)}) %collective-permute-start.41) | collective-permute-done | bytes 65568 | tf_op jit(solution)/shard_map/ppermute | solution.py:22
  161.0 1.5 collective-permute-done.42
  162.5 2.1 %collective-permute-done.43 = f32[10,1,16,128]{3,2,1,0:T(8,128)S(1)} collective-permute-done((f32[10,1,16,128]{3,2,1,0:T(8,128)S(1)}, f32[10,1,16,128]{3,2,1,0:T(8,128)S(1)}, u32[]{:S(2)}, u32[]{:S(2)}) %collective-permute-start.43) | collective-permute-done | bytes 81952 | tf_op jit(solution)/shard_map/ppermute | solution.py:22
  164.6 1.3 fusion.9
  (134 shorter events, 11.8 us)
Async XLA Ops:
  0.6 80.2 %copy-start = (bf16[4,4,2,128,128]{4,3,2,1,0:T(8,128)(2,1)S(1)}, bf16[4,4,2,128,128]{4,3,2,1,0:T(8,128)(2,1)}, u32[]{:S(2)}) copy-start(bf16[4,4,2,128,128]{4,3,2,1,0:T(8,128)(2,1)} %param.31) | copy-start | bytes 3145732
  7.7 9.4 %collective-permute-start.1 = (f32[1,4,16,128]{3,2,1,0:T(8,128)S(1)}, f32[1,4,16,128]{3,2,1,0:T(8,128)S(1)}, u32[]{:S(2)}, u32[]{:S(2)}) collective-permute-start(f32[1,4,16,128]{3,2,1,0:T(8,128)S(1)} %bitcast.49), channel_id=1, source_target_pairs={{0,4},{4,8},{8,12},{12,16},{16,20},{20,24},{24,28},{28,0},{1,5},{5... | collective-permute-start | bytes 98312 | tf_op jit(solution)/shard_map/ppermute | solution.py:22
  9.7 7.4 %collective-permute-start = (f32[1,4,16,128]{3,2,1,0:T(8,128)S(1)}, f32[1,4,16,128]{3,2,1,0:T(8,128)S(1)}, u32[]{:S(2)}, u32[]{:S(2)}) collective-permute-start(f32[1,4,16,128]{3,2,1,0:T(8,128)S(1)} %bitcast.50), channel_id=1, source_target_pairs={{4,0},{8,4},{12,8},{16,12},{20,16},{24,20},{28,24},{0,28},{5,1},{9... | collective-permute-start | bytes 98312 | tf_op jit(solution)/shard_map/ppermute | solution.py:23
  17.2 6.7 %collective-permute-start.3 = (f32[1,4,16,128]{3,2,1,0:T(8,128)S(1)}, f32[1,4,16,128]{3,2,1,0:T(8,128)S(1)}, u32[]{:S(2)}, u32[]{:S(2)}) collective-permute-start(f32[1,4,16,128]{3,2,1,0:T(8,128)S(1)} %get-tuple-element.28), channel_id=1, source_target_pairs={{0,4},{4,8},{8,12},{12,16},{16,20},{20,24},{24,28},{28,0},{1,5},{5... | collective-permute-start | bytes 98312 | tf_op jit(solution)/shard_map/ppermute | solution.py:22
  17.3 6.6 %collective-permute-start.2 = (f32[1,4,16,128]{3,2,1,0:T(8,128)S(1)}, f32[1,4,16,128]{3,2,1,0:T(8,128)S(1)}, u32[]{:S(2)}, u32[]{:S(2)}) collective-permute-start(f32[1,4,16,128]{3,2,1,0:T(8,128)S(1)} %get-tuple-element.28), channel_id=1, source_target_pairs={{4,0},{8,4},{12,8},{16,12},{20,16},{24,20},{28,24},{0,28},{5,1},{9... | collective-permute-start | bytes 98312 | tf_op jit(solution)/shard_map/ppermute | solution.py:23
  24.0 6.7 %collective-permute-start.5 = (f32[1,4,16,128]{3,2,1,0:T(8,128)S(1)}, f32[1,4,16,128]{3,2,1,0:T(8,128)S(1)}, u32[]{:S(2)}, u32[]{:S(2)}) collective-permute-start(f32[1,4,16,128]{3,2,1,0:T(8,128)S(1)} %get-tuple-element.26), channel_id=1, source_target_pairs={{0,4},{4,8},{8,12},{12,16},{16,20},{20,24},{24,28},{28,0},{1,5},{5... | collective-permute-start | bytes 98312 | tf_op jit(solution)/shard_map/ppermute | solution.py:22
  24.0 6.6 %collective-permute-start.4 = (f32[1,4,16,128]{3,2,1,0:T(8,128)S(1)}, f32[1,4,16,128]{3,2,1,0:T(8,128)S(1)}, u32[]{:S(2)}, u32[]{:S(2)}) collective-permute-start(f32[1,4,16,128]{3,2,1,0:T(8,128)S(1)} %get-tuple-element.26), channel_id=1, source_target_pairs={{4,0},{8,4},{12,8},{16,12},{20,16},{24,20},{28,24},{0,28},{5,1},{9... | collective-permute-start | bytes 98312 | tf_op jit(solution)/shard_map/ppermute | solution.py:23
  30.8 6.3 %collective-permute-start.7 = (bf16[1,4,16,128]{3,2,1,0:T(8,128)(2,1)S(1)}, bf16[1,4,16,128]{3,2,1,0:T(8,128)(2,1)S(1)}, u32[]{:S(2)}, u32[]{:S(2)}) collective-permute-start(bf16[1,4,16,128]{3,2,1,0:T(8,128)(2,1)S(1)} %get-tuple-element.24), channel_id=1, source_target_pairs={{4,0},{8,4},{12,8},{16,12},{20,16},{24,20},{28,24},{0,28},{5,1},{9... | collective-permute-start | bytes 49160 | tf_op jit(solution)/shard_map/ppermute | solution.py:23
  35.6 6.4 %collective-permute-start.6 = (bf16[1,4,16,128]{3,2,1,0:T(8,128)(2,1)S(1)}, bf16[1,4,16,128]{3,2,1,0:T(8,128)(2,1)S(1)}, u32[]{:S(2)}, u32[]{:S(2)}) collective-permute-start(bf16[1,4,16,128]{3,2,1,0:T(8,128)(2,1)S(1)} %get-tuple-element.24), channel_id=1, source_target_pairs={{0,4},{4,8},{8,12},{12,16},{16,20},{20,24},{24,28},{28,0},{1,5},{5... | collective-permute-start | bytes 49160 | tf_op jit(solution)/shard_map/ppermute | solution.py:22
  51.0 4.4 %collective-permute-start.8 = (f32[1,8,16,128]{3,2,1,0:T(8,128)S(1)}, f32[1,8,16,128]{3,2,1,0:T(8,128)S(1)}, u32[]{:S(2)}, u32[]{:S(2)}) collective-permute-start(f32[1,8,16,128]{3,2,1,0:T(8,128)S(1)} %get-tuple-element.54), channel_id=1, source_target_pairs={{4,0},{8,4},{12,8},{16,12},{20,16},{24,20},{28,24},{0,28},{5,1},{9... | collective-permute-start | bytes 196616 | tf_op jit(solution)/shard_map/ppermute | solution.py:23
  51.1 7.1 %collective-permute-start.9 = (f32[1,8,16,128]{3,2,1,0:T(8,128)S(1)}, f32[1,8,16,128]{3,2,1,0:T(8,128)S(1)}, u32[]{:S(2)}, u32[]{:S(2)}) collective-permute-start(f32[1,8,16,128]{3,2,1,0:T(8,128)S(1)} %get-tuple-element.55), channel_id=1, source_target_pairs={{0,4},{4,8},{8,12},{12,16},{16,20},{20,24},{24,28},{28,0},{1,5},{5... | collective-permute-start | bytes 196616 | tf_op jit(solution)/shard_map/ppermute | solution.py:22
  58.2 22.6 %copy-start.4 = (f32[4,4,16,128]{3,2,1,0:T(8,128)S(1)}, f32[4,4,16,128]{3,2,1,0:T(8,128)}, u32[]{:S(2)}) copy-start(f32[4,4,16,128]{3,2,1,0:T(8,128)} %param.23) | copy-start | bytes 393220
  58.6 4.3 %collective-permute-start.10 = (f32[1,8,16,128]{3,2,1,0:T(8,128)S(1)}, f32[1,8,16,128]{3,2,1,0:T(8,128)S(1)}, u32[]{:S(2)}, u32[]{:S(2)}) collective-permute-start(f32[1,8,16,128]{3,2,1,0:T(8,128)S(1)} %get-tuple-element.98), channel_id=1, source_target_pairs={{4,0},{8,4},{12,8},{16,12},{20,16},{24,20},{28,24},{0,28},{5,1},{9... | collective-permute-start | bytes 196616 | tf_op jit(solution)/shard_map/ppermute | solution.py:23
  58.9 7.0 %collective-permute-start.11 = (f32[1,8,16,128]{3,2,1,0:T(8,128)S(1)}, f32[1,8,16,128]{3,2,1,0:T(8,128)S(1)}, u32[]{:S(2)}, u32[]{:S(2)}) collective-permute-start(f32[1,8,16,128]{3,2,1,0:T(8,128)S(1)} %get-tuple-element.99), channel_id=1, source_target_pairs={{0,4},{4,8},{8,12},{12,16},{16,20},{20,24},{24,28},{28,0},{1,5},{5... | collective-permute-start | bytes 196616 | tf_op jit(solution)/shard_map/ppermute | solution.py:22
  65.8 26.2 %copy-start.3 = (f32[4,4,16,128]{3,2,1,0:T(8,128)S(1)}, f32[4,4,16,128]{3,2,1,0:T(8,128)}, u32[]{:S(2)}) copy-start(f32[4,4,16,128]{3,2,1,0:T(8,128)} %param.19) | copy-start | bytes 393220
  66.2 5.0 %collective-permute-start.12 = (f32[1,8,16,128]{3,2,1,0:T(8,128)S(1)}, f32[1,8,16,128]{3,2,1,0:T(8,128)S(1)}, u32[]{:S(2)}, u32[]{:S(2)}) collective-permute-start(f32[1,8,16,128]{3,2,1,0:T(8,128)S(1)} %get-tuple-element.88), channel_id=1, source_target_pairs={{4,0},{8,4},{12,8},{16,12},{20,16},{24,20},{28,24},{0,28},{5,1},{9... | collective-permute-start | bytes 196616 | tf_op jit(solution)/shard_map/ppermute | solution.py:23
  66.3 7.0 %collective-permute-start.13 = (f32[1,8,16,128]{3,2,1,0:T(8,128)S(1)}, f32[1,8,16,128]{3,2,1,0:T(8,128)S(1)}, u32[]{:S(2)}, u32[]{:S(2)}) collective-permute-start(f32[1,8,16,128]{3,2,1,0:T(8,128)S(1)} %get-tuple-element.89), channel_id=1, source_target_pairs={{0,4},{4,8},{8,12},{12,16},{16,20},{20,24},{24,28},{28,0},{1,5},{5... | collective-permute-start | bytes 196616 | tf_op jit(solution)/shard_map/ppermute | solution.py:22
  73.5 6.7 %collective-permute-start.14 = (bf16[1,8,16,128]{3,2,1,0:T(8,128)(2,1)S(1)}, bf16[1,8,16,128]{3,2,1,0:T(8,128)(2,1)S(1)}, u32[]{:S(2)}, u32[]{:S(2)}) collective-permute-start(bf16[1,8,16,128]{3,2,1,0:T(8,128)(2,1)S(1)} %get-tuple-element.122), channel_id=1, source_target_pairs={{0,4},{4,8},{8,12},{12,16},{16,20},{20,24},{24,28},{28,0},{1,5},{5... | collective-permute-start | bytes 98312 | tf_op jit(solution)/shard_map/ppermute | solution.py:22
  73.6 6.6 %collective-permute-start.15 = (bf16[1,8,16,128]{3,2,1,0:T(8,128)(2,1)S(1)}, bf16[1,8,16,128]{3,2,1,0:T(8,128)(2,1)S(1)}, u32[]{:S(2)}, u32[]{:S(2)}) collective-permute-start(bf16[1,8,16,128]{3,2,1,0:T(8,128)(2,1)S(1)} %get-tuple-element.123), channel_id=1, source_target_pairs={{4,0},{8,4},{12,8},{16,12},{20,16},{24,20},{28,24},{0,28},{5,1},{9... | collective-permute-start | bytes 98312 | tf_op jit(solution)/shard_map/ppermute | solution.py:23
  81.2 6.8 %collective-permute-start.17 = (f32[1,4,16,128]{3,2,1,0:T(8,128)S(1)}, f32[1,4,16,128]{3,2,1,0:T(8,128)S(1)}, u32[]{:S(2)}, u32[]{:S(2)}) collective-permute-start(f32[1,4,16,128]{3,2,1,0:T(8,128)S(1)} %get-tuple-element.82), channel_id=1, source_target_pairs={{0,4},{4,8},{8,12},{12,16},{16,20},{20,24},{24,28},{28,0},{1,5},{5... | collective-permute-start | bytes 98312 | tf_op jit(solution)/shard_map/ppermute | solution.py:22
  81.3 6.7 %collective-permute-start.16 = (f32[1,4,16,128]{3,2,1,0:T(8,128)S(1)}, f32[1,4,16,128]{3,2,1,0:T(8,128)S(1)}, u32[]{:S(2)}, u32[]{:S(2)}) collective-permute-start(f32[1,4,16,128]{3,2,1,0:T(8,128)S(1)} %get-tuple-element.83), channel_id=1, source_target_pairs={{4,0},{8,4},{12,8},{16,12},{20,16},{24,20},{28,24},{0,28},{5,1},{9... | collective-permute-start | bytes 98312 | tf_op jit(solution)/shard_map/ppermute | solution.py:23
  88.0 1.8 %collective-permute-start.18 = (f32[6,1,16,128]{3,2,1,0:T(8,128)S(1)}, f32[6,1,16,128]{3,2,1,0:T(8,128)S(1)}, u32[]{:S(2)}, u32[]{:S(2)}) collective-permute-start(f32[6,1,16,128]{3,2,1,0:T(8,128)S(1)} %get-tuple-element.68), channel_id=1, source_target_pairs={{1,0},{2,1},{3,2},{0,3},{5,4},{6,5},{7,6},{4,7},{9,8},{10,9},{11,1... | collective-permute-start | bytes 147464 | tf_op jit(solution)/shard_map/ppermute | solution.py:23
  88.1 3.9 %collective-permute-start.19 = (f32[6,1,16,128]{3,2,1,0:T(8,128)S(1)}, f32[6,1,16,128]{3,2,1,0:T(8,128)S(1)}, u32[]{:S(2)}, u32[]{:S(2)}) collective-permute-start(f32[6,1,16,128]{3,2,1,0:T(8,128)S(1)} %get-tuple-element.69), channel_id=1, source_target_pairs={{0,1},{1,2},{2,3},{3,0},{4,5},{5,6},{6,7},{7,4},{8,9},{9,10},{10,1... | collective-permute-start | bytes 147464 | tf_op jit(solution)/shard_map/ppermute | solution.py:22
  92.0 32.5 %copy-start.2 = (f32[8,8,16,128]{3,2,1,0:T(8,128)S(1)}, f32[8,8,16,128]{3,2,1,0:T(8,128)}, u32[]{:S(2)}) copy-start(f32[8,8,16,128]{3,2,1,0:T(8,128)} %param.22) | copy-start | bytes 1572868
  92.2 6.7 %collective-permute-start.21 = (f32[1,4,16,128]{3,2,1,0:T(8,128)S(1)}, f32[1,4,16,128]{3,2,1,0:T(8,128)S(1)}, u32[]{:S(2)}, u32[]{:S(2)}) collective-permute-start(f32[1,4,16,128]{3,2,1,0:T(8,128)S(1)} %get-tuple-element.76), channel_id=1, source_target_pairs={{0,4},{4,8},{8,12},{12,16},{16,20},{20,24},{24,28},{28,0},{1,5},{5... | collective-permute-start | bytes 98312 | tf_op jit(solution)/shard_map/ppermute | solution.py:22
  92.2 6.7 %collective-permute-start.20 = (f32[1,4,16,128]{3,2,1,0:T(8,128)S(1)}, f32[1,4,16,128]{3,2,1,0:T(8,128)S(1)}, u32[]{:S(2)}, u32[]{:S(2)}) collective-permute-start(f32[1,4,16,128]{3,2,1,0:T(8,128)S(1)} %get-tuple-element.77), channel_id=1, source_target_pairs={{4,0},{8,4},{12,8},{16,12},{20,16},{24,20},{28,24},{0,28},{5,1},{9... | collective-permute-start | bytes 98312 | tf_op jit(solution)/shard_map/ppermute | solution.py:23
  98.9 1.8 %collective-permute-start.22 = (f32[6,1,16,128]{3,2,1,0:T(8,128)S(1)}, f32[6,1,16,128]{3,2,1,0:T(8,128)S(1)}, u32[]{:S(2)}, u32[]{:S(2)}) collective-permute-start(f32[6,1,16,128]{3,2,1,0:T(8,128)S(1)} %get-tuple-element.66), channel_id=1, source_target_pairs={{1,0},{2,1},{3,2},{0,3},{5,4},{6,5},{7,6},{4,7},{9,8},{10,9},{11,1... | collective-permute-start | bytes 147464 | tf_op jit(solution)/shard_map/ppermute | solution.py:23
  99.0 3.6 %collective-permute-start.23 = (f32[6,1,16,128]{3,2,1,0:T(8,128)S(1)}, f32[6,1,16,128]{3,2,1,0:T(8,128)S(1)}, u32[]{:S(2)}, u32[]{:S(2)}) collective-permute-start(f32[6,1,16,128]{3,2,1,0:T(8,128)S(1)} %get-tuple-element.67), channel_id=1, source_target_pairs={{0,1},{1,2},{2,3},{3,0},{4,5},{5,6},{6,7},{7,4},{8,9},{9,10},{10,1... | collective-permute-start | bytes 147464 | tf_op jit(solution)/shard_map/ppermute | solution.py:22
  102.7 6.7 %collective-permute-start.25 = (f32[1,4,16,128]{3,2,1,0:T(8,128)S(1)}, f32[1,4,16,128]{3,2,1,0:T(8,128)S(1)}, u32[]{:S(2)}, u32[]{:S(2)}) collective-permute-start(f32[1,4,16,128]{3,2,1,0:T(8,128)S(1)} %get-tuple-element.70), channel_id=1, source_target_pairs={{0,4},{4,8},{8,12},{12,16},{16,20},{20,24},{24,28},{28,0},{1,5},{5... | collective-permute-start | bytes 98312 | tf_op jit(solution)/shard_map/ppermute | solution.py:22
  102.8 6.7 %collective-permute-start.24 = (f32[1,4,16,128]{3,2,1,0:T(8,128)S(1)}, f32[1,4,16,128]{3,2,1,0:T(8,128)S(1)}, u32[]{:S(2)}, u32[]{:S(2)}) collective-permute-start(f32[1,4,16,128]{3,2,1,0:T(8,128)S(1)} %get-tuple-element.71), channel_id=1, source_target_pairs={{4,0},{8,4},{12,8},{16,12},{20,16},{24,20},{28,24},{0,28},{5,1},{9... | collective-permute-start | bytes 98312 | tf_op jit(solution)/shard_map/ppermute | solution.py:23
  109.4 1.8 %collective-permute-start.26 = (f32[6,1,16,128]{3,2,1,0:T(8,128)S(1)}, f32[6,1,16,128]{3,2,1,0:T(8,128)S(1)}, u32[]{:S(2)}, u32[]{:S(2)}) collective-permute-start(f32[6,1,16,128]{3,2,1,0:T(8,128)S(1)} %get-tuple-element.64), channel_id=1, source_target_pairs={{1,0},{2,1},{3,2},{0,3},{5,4},{6,5},{7,6},{4,7},{9,8},{10,9},{11,1... | collective-permute-start | bytes 147464 | tf_op jit(solution)/shard_map/ppermute | solution.py:23
  109.5 3.6 %collective-permute-start.27 = (f32[6,1,16,128]{3,2,1,0:T(8,128)S(1)}, f32[6,1,16,128]{3,2,1,0:T(8,128)S(1)}, u32[]{:S(2)}, u32[]{:S(2)}) collective-permute-start(f32[6,1,16,128]{3,2,1,0:T(8,128)S(1)} %get-tuple-element.65), channel_id=1, source_target_pairs={{0,1},{1,2},{2,3},{3,0},{4,5},{5,6},{6,7},{7,4},{8,9},{9,10},{10,1... | collective-permute-start | bytes 147464 | tf_op jit(solution)/shard_map/ppermute | solution.py:22
  113.9 6.5 %collective-permute-start.28 = (bf16[1,4,16,128]{3,2,1,0:T(8,128)(2,1)S(1)}, bf16[1,4,16,128]{3,2,1,0:T(8,128)(2,1)S(1)}, u32[]{:S(2)}, u32[]{:S(2)}) collective-permute-start(bf16[1,4,16,128]{3,2,1,0:T(8,128)(2,1)S(1)} %get-tuple-element.120), channel_id=1, source_target_pairs={{0,4},{4,8},{8,12},{12,16},{16,20},{20,24},{24,28},{28,0},{1,5},{5... | collective-permute-start | bytes 49160 | tf_op jit(solution)/shard_map/ppermute | solution.py:22
  113.9 6.5 %collective-permute-start.29 = (bf16[1,4,16,128]{3,2,1,0:T(8,128)(2,1)S(1)}, bf16[1,4,16,128]{3,2,1,0:T(8,128)(2,1)S(1)}, u32[]{:S(2)}, u32[]{:S(2)}) collective-permute-start(bf16[1,4,16,128]{3,2,1,0:T(8,128)(2,1)S(1)} %get-tuple-element.121), channel_id=1, source_target_pairs={{4,0},{8,4},{12,8},{16,12},{20,16},{24,20},{28,24},{0,28},{5,1},{9... | collective-permute-start | bytes 49160 | tf_op jit(solution)/shard_map/ppermute | solution.py:23
  120.5 3.3 %collective-permute-start.30 = (bf16[6,1,16,128]{3,2,1,0:T(8,128)(2,1)S(1)}, bf16[6,1,16,128]{3,2,1,0:T(8,128)(2,1)S(1)}, u32[]{:S(2)}, u32[]{:S(2)}) collective-permute-start(bf16[6,1,16,128]{3,2,1,0:T(8,128)(2,1)S(1)} %get-tuple-element.108), channel_id=1, source_target_pairs={{0,1},{1,2},{2,3},{3,0},{4,5},{5,6},{6,7},{7,4},{8,9},{9,10},{10,1... | collective-permute-start | bytes 73736 | tf_op jit(solution)/shard_map/ppermute | solution.py:22
  120.5 3.3 %collective-permute-start.31 = (bf16[6,1,16,128]{3,2,1,0:T(8,128)(2,1)S(1)}, bf16[6,1,16,128]{3,2,1,0:T(8,128)(2,1)S(1)}, u32[]{:S(2)}, u32[]{:S(2)}) collective-permute-start(bf16[6,1,16,128]{3,2,1,0:T(8,128)(2,1)S(1)} %get-tuple-element.109), channel_id=1, source_target_pairs={{1,0},{2,1},{3,2},{0,3},{5,4},{6,5},{7,6},{4,7},{9,8},{10,9},{11,1... | collective-permute-start | bytes 73736 | tf_op jit(solution)/shard_map/ppermute | solution.py:23
  124.5 16.0 %copy-start.1 = (f32[8,8,16,128]{3,2,1,0:T(8,128)S(1)}, f32[8,8,16,128]{3,2,1,0:T(8,128)}, u32[]{:S(2)}) copy-start(f32[8,8,16,128]{3,2,1,0:T(8,128)} %param.18) | copy-start | bytes 1572868
  128.0 7.3 %collective-permute-start.33 = (f32[1,8,16,128]{3,2,1,0:T(8,128)S(1)}, f32[1,8,16,128]{3,2,1,0:T(8,128)S(1)}, u32[]{:S(2)}, u32[]{:S(2)}) collective-permute-start(f32[1,8,16,128]{3,2,1,0:T(8,128)S(1)} %get-tuple-element.48), channel_id=1, source_target_pairs={{0,4},{4,8},{8,12},{12,16},{16,20},{20,24},{24,28},{28,0},{1,5},{5... | collective-permute-start | bytes 196616 | tf_op jit(solution)/shard_map/ppermute | solution.py:22
  128.1 7.3 %collective-permute-start.32 = (f32[1,8,16,128]{3,2,1,0:T(8,128)S(1)}, f32[1,8,16,128]{3,2,1,0:T(8,128)S(1)}, u32[]{:S(2)}, u32[]{:S(2)}) collective-permute-start(f32[1,8,16,128]{3,2,1,0:T(8,128)S(1)} %get-tuple-element.49), channel_id=1, source_target_pairs={{4,0},{8,4},{12,8},{16,12},{20,16},{24,20},{28,24},{0,28},{5,1},{9... | collective-permute-start | bytes 196616 | tf_op jit(solution)/shard_map/ppermute | solution.py:23
  135.3 3.2 %collective-permute-start.34 = (f32[10,1,16,128]{3,2,1,0:T(8,128)S(1)}, f32[10,1,16,128]{3,2,1,0:T(8,128)S(1)}, u32[]{:S(2)}, u32[]{:S(2)}) collective-permute-start(f32[10,1,16,128]{3,2,1,0:T(8,128)S(1)} %get-tuple-element.34), channel_id=1, source_target_pairs={{1,0},{2,1},{3,2},{0,3},{5,4},{6,5},{7,6},{4,7},{9,8},{10,9},{11,1... | collective-permute-start | bytes 245768 | tf_op jit(solution)/shard_map/ppermute | solution.py:23
  136.2 4.3 %collective-permute-start.35 = (f32[10,1,16,128]{3,2,1,0:T(8,128)S(1)}, f32[10,1,16,128]{3,2,1,0:T(8,128)S(1)}, u32[]{:S(2)}, u32[]{:S(2)}) collective-permute-start(f32[10,1,16,128]{3,2,1,0:T(8,128)S(1)} %get-tuple-element.35), channel_id=1, source_target_pairs={{0,1},{1,2},{2,3},{3,0},{4,5},{5,6},{6,7},{7,4},{8,9},{9,10},{10,1... | collective-permute-start | bytes 245768 | tf_op jit(solution)/shard_map/ppermute | solution.py:22
  141.0 7.3 %collective-permute-start.37 = (f32[1,8,16,128]{3,2,1,0:T(8,128)S(1)}, f32[1,8,16,128]{3,2,1,0:T(8,128)S(1)}, u32[]{:S(2)}, u32[]{:S(2)}) collective-permute-start(f32[1,8,16,128]{3,2,1,0:T(8,128)S(1)} %get-tuple-element.42), channel_id=1, source_target_pairs={{0,4},{4,8},{8,12},{12,16},{16,20},{20,24},{24,28},{28,0},{1,5},{5... | collective-permute-start | bytes 196616 | tf_op jit(solution)/shard_map/ppermute | solution.py:22
  141.1 7.2 %collective-permute-start.36 = (f32[1,8,16,128]{3,2,1,0:T(8,128)S(1)}, f32[1,8,16,128]{3,2,1,0:T(8,128)S(1)}, u32[]{:S(2)}, u32[]{:S(2)}) collective-permute-start(f32[1,8,16,128]{3,2,1,0:T(8,128)S(1)} %get-tuple-element.43), channel_id=1, source_target_pairs={{4,0},{8,4},{12,8},{16,12},{20,16},{24,20},{28,24},{0,28},{5,1},{9... | collective-permute-start | bytes 196616 | tf_op jit(solution)/shard_map/ppermute | solution.py:23
  148.3 2.5 %collective-permute-start.38 = (f32[10,1,16,128]{3,2,1,0:T(8,128)S(1)}, f32[10,1,16,128]{3,2,1,0:T(8,128)S(1)}, u32[]{:S(2)}, u32[]{:S(2)}) collective-permute-start(f32[10,1,16,128]{3,2,1,0:T(8,128)S(1)} %get-tuple-element.32), channel_id=1, source_target_pairs={{1,0},{2,1},{3,2},{0,3},{5,4},{6,5},{7,6},{4,7},{9,8},{10,9},{11,1... | collective-permute-start | bytes 245768 | tf_op jit(solution)/shard_map/ppermute | solution.py:23
  148.4 4.2 %collective-permute-start.39 = (f32[10,1,16,128]{3,2,1,0:T(8,128)S(1)}, f32[10,1,16,128]{3,2,1,0:T(8,128)S(1)}, u32[]{:S(2)}, u32[]{:S(2)}) collective-permute-start(f32[10,1,16,128]{3,2,1,0:T(8,128)S(1)} %get-tuple-element.33), channel_id=1, source_target_pairs={{0,1},{1,2},{2,3},{3,0},{4,5},{5,6},{6,7},{7,4},{8,9},{9,10},{10,1... | collective-permute-start | bytes 245768 | tf_op jit(solution)/shard_map/ppermute | solution.py:22
  153.1 7.1 %collective-permute-start.41 = (f32[1,8,16,128]{3,2,1,0:T(8,128)S(1)}, f32[1,8,16,128]{3,2,1,0:T(8,128)S(1)}, u32[]{:S(2)}, u32[]{:S(2)}) collective-permute-start(f32[1,8,16,128]{3,2,1,0:T(8,128)S(1)} %get-tuple-element.40), channel_id=1, source_target_pairs={{0,4},{4,8},{8,12},{12,16},{16,20},{20,24},{24,28},{28,0},{1,5},{5... | collective-permute-start | bytes 196616 | tf_op jit(solution)/shard_map/ppermute | solution.py:22
  153.2 7.0 %collective-permute-start.40 = (f32[1,8,16,128]{3,2,1,0:T(8,128)S(1)}, f32[1,8,16,128]{3,2,1,0:T(8,128)S(1)}, u32[]{:S(2)}, u32[]{:S(2)}) collective-permute-start(f32[1,8,16,128]{3,2,1,0:T(8,128)S(1)} %get-tuple-element.41), channel_id=1, source_target_pairs={{4,0},{8,4},{12,8},{16,12},{20,16},{24,20},{28,24},{0,28},{5,1},{9... | collective-permute-start | bytes 196616 | tf_op jit(solution)/shard_map/ppermute | solution.py:23
  160.2 2.3 %collective-permute-start.42 = (f32[10,1,16,128]{3,2,1,0:T(8,128)S(1)}, f32[10,1,16,128]{3,2,1,0:T(8,128)S(1)}, u32[]{:S(2)}, u32[]{:S(2)}) collective-permute-start(f32[10,1,16,128]{3,2,1,0:T(8,128)S(1)} %get-tuple-element.30), channel_id=1, source_target_pairs={{1,0},{2,1},{3,2},{0,3},{5,4},{6,5},{7,6},{4,7},{9,8},{10,9},{11,1... | collective-permute-start | bytes 245768 | tf_op jit(solution)/shard_map/ppermute | solution.py:23
  160.3 4.4 %collective-permute-start.43 = (f32[10,1,16,128]{3,2,1,0:T(8,128)S(1)}, f32[10,1,16,128]{3,2,1,0:T(8,128)S(1)}, u32[]{:S(2)}, u32[]{:S(2)}) collective-permute-start(f32[10,1,16,128]{3,2,1,0:T(8,128)S(1)} %get-tuple-element.31), channel_id=1, source_target_pairs={{0,1},{1,2},{2,3},{3,0},{4,5},{5,6},{6,7},{7,4},{8,9},{9,10},{10,1... | collective-permute-start | bytes 245768 | tf_op jit(solution)/shard_map/ppermute | solution.py:22
where the time goes:
time: 166 us
  starting transfers between devices  70.2 us (42%)
  waiting for transfers between devices  60.8 us (37%)
  blocking collectives  12.5 us (8%)
  other arithmetic  9.63 us (6%)
  local copies, waits for them, and re-layouts  6.72 us (4%)
  matrix products  4.93 us (3%)
    ppermute x22, starting transfers between devices, padded(): after = lax.ppermute(initial, axis, down)  59.3 us
    ppermute x22, waiting for transfers between devices, padded(): before = lax.ppermute(last, axis, up)  43.3 us
    ppermute x22, waiting for transfers between devices, padded(): after = lax.ppermute(initial, axis, down)  17.6 us
    all_gather x2, blocking collectives, gathered_smooth(): lax.all_gather(pack_level(source, initial, diagonal), 'gy', axis=1, tiled...  12.5 us
    ppermute x22, starting transfers between devices, padded(): before = lax.ppermute(last, axis, up)  10.9 us
    dot_general x3, matrix products, prolong_local(): jnp.einsum('abkrj,abkij->abri', picked_lines, blocks, preferred_element_t...  4.93 us
  transfers between devices with their start and end apart: 44, of which 31 were waited for; matrix products, arithmetic and copies ran while one was open for 5% of the time, Pallas kernels for 0%

commit v1 on v0

v1 whole, which is shorter than its diff:
```python
from functools import partial

import jax
import jax.numpy as jnp
from jax import lax
from jax.experimental import pallas as pl
from jax.experimental.pallas import tpu as pltpu
from jax.sharding import PartitionSpec as P

DEGREE = 3
LEVELS = 4
REACH = DEGREE

upper_edge = 14.0
lower_edge = upper_edge / 8.0


def coefficients():
    centre = (upper_edge + lower_edge) / 2.0
    half_width = (upper_edge - lower_edge) / 2.0
    ratio = centre / half_width
    factor = 1.0 / ratio
    steps = []
    for _ in range(DEGREE - 1):
        following = 1.0 / (2.0 * ratio - factor)
        steps.append((following * factor, 2.0 * following / half_width))
        factor = following
    return 1.0 / centre, steps


def span(offset, length, reach):
    low = max(offset * length, -reach)
    high = min((offset + 1) * length, length + reach)
    return low, high


def plan(nx, ny, reach, box):
    out = []
    far_x, far_y = -(-reach // nx), -(-reach // ny)
    for ox in range(-far_x, far_x + 1):
        for oy in range(-far_y, far_y + 1):
            if ox == 0 and oy == 0:
                continue
            limit = reach - 1 if (ox and oy and not box) else reach
            rows, cols = span(-ox, nx, limit), span(-oy, ny, limit)
            if rows[0] >= rows[1] or cols[0] >= cols[1]:
                continue
            far = (nx * (abs(ox) - 1) + 1 if ox else 0) + (ny * (abs(oy) - 1) + 1 if oy else 0)
            if not box and far > reach:
                continue
            source = (rows[0] + ox * nx, cols[0] + oy * ny)
            out.append((ox, oy, source, (rows[0], cols[0]), (rows[1] - rows[0], cols[1] - cols[0])))
    out.sort(key=lambda m: (abs(m[0]) + abs(m[1]), m))
    return out


def modulo(value, size):
    if size & (size - 1) == 0:
        return jnp.bitwise_and(value, size - 1)
    return lax.rem(value, size)


def quotient(value, size):
    if size & (size - 1) == 0:
        return jnp.right_shift(value, size.bit_length() - 1)
    return lax.div(value, size)


class Counter:
    def __init__(self):
        self.used = 0

    def take(self):
        self.used += 1
        return self.used - 1


def message_count(dims):
    total = 0
    for level, (nx, ny) in enumerate(dims):
        total += len(plan(nx, ny, REACH, False)) + 2 * len(plan(nx, ny, REACH - 1, False))
        if level:
            total += len(plan(nx, ny, 1, True))
    return total


def partners(dims, peers):
    found = set()
    for level, (nx, ny) in enumerate(dims):
        for m in plan(nx, ny, REACH, False) + plan(nx, ny, 1, True):
            found.add((m[0] % peers[0], m[1] % peers[1]))
            found.add((-m[0] % peers[0], -m[1] % peers[1]))
    return sorted(found)


def kernel(dims, peers, *refs):
    sources, guesses, shifts = refs[0:4], refs[4:8], refs[8:12]
    blocks, links = refs[12:15], refs[15:18]
    outs = refs[18:22]
    U, S, D, R, P0, P1, O = (refs[22 + 4 * k : 26 + 4 * k] for k in range(7))
    B, C, H = refs[50:53], refs[53:56], refs[56:60]
    local_sem, send_sem, recv_sem = refs[60:63]
    gz, gy = lax.axis_index("gz"), lax.axis_index("gy")

    def at(ox, oy):
        return (lax.rem(gz + (ox % peers[0]), peers[0]), lax.rem(gy + (oy % peers[1]), peers[1]))

    barrier = pltpu.get_barrier_semaphore()
    company = partners(dims, peers)
    for ox, oy in company:
        pl.semaphore_signal(barrier, inc=1, device_id=at(ox, oy), device_id_type=pl.DeviceIdType.MESH)

    local = Counter()

    def fetch(source, target):
        copy = pltpu.make_async_copy(source, target, local_sem.at[local.take()])
        copy.start()
        return copy

    def own(ref, level, reach):
        nx, ny = dims[level]
        return ref.at[pl.ds(reach, nx), pl.ds(reach, ny)]

    loads = [None] * LEVELS
    for level in reversed(range(LEVELS)):
        loads[level] = [
            fetch(shifts[level], H[level]),
            fetch(guesses[level], own(U[level], level, REACH)),
            fetch(sources[level], own(S[level], level, REACH - 1)),
        ]
    block_loads = [None] * (LEVELS - 1)
    for level in reversed(range(LEVELS - 1)):
        block_loads[level] = fetch(blocks[level], B[level])

    for level in reversed(range(LEVELS)):
        nx, ny = dims[level]
        for copy in loads[level]:
            copy.wait()
        for i in range(nx):
            for j in range(ny):
                D[level][i + REACH - 1, j + REACH - 1] = 6.0 + H[level][i, pl.ds(j, 1)]

    pl.semaphore_wait(barrier, len(company))

    counter = Counter()
    pending = []

    def exchange(ref, level, reach, box=False):
        copies = []
        for ox, oy, source, target, size in plan(*dims[level], reach, box):
            index = counter.take()
            copy = pltpu.make_async_remote_copy(
                src_ref=ref.at[pl.ds(source[0] + reach, size[0]), pl.ds(source[1] + reach, size[1])],
                dst_ref=ref.at[pl.ds(target[0] + reach, size[0]), pl.ds(target[1] + reach, size[1])],
                send_sem=send_sem.at[index],
                recv_sem=recv_sem.at[index],
                device_id=at(ox, oy),
                device_id_type=pl.DeviceIdType.MESH,
            )
            copy.start()
            copies.append(copy)
        pending.extend(copies)
        return copies

    first, steps = coefficients()

    def rows(count, body):
        if count <= 5:
            for i in range(count):
                body(i)
        else:
            lax.fori_loop(0, count, lambda i, c: (body(i), c)[1], 0)

    def operate(ref, diagonal, i, count):
        wide = ref[i + 1]
        middle = wide[1 : count + 1]
        beside = wide[0:count] + wide[2 : count + 2]
        beside = beside + (ref[i, pl.ds(1, count)] + ref[i + 2, pl.ds(1, count)])
        beside = beside + (pltpu.roll(middle, 1, 2) + pltpu.roll(middle, middle.shape[2] - 1, 2))
        return diagonal * middle - beside

    def smooth(level):
        nx, ny = dims[level]
        u, s, d, r, p0, p1, o = (x[level] for x in (U, S, D, R, P0, P1, O))

        def start(i):
            residual = s[i] - operate(u, d[i], i, ny + 4)
            r[i] = residual
            p0[i] = residual * first

        rows(nx + 4, start)
        ahead, along = steps[0]

        def second(i):
            residual = r[i + 1, pl.ds(1, ny + 2)] - operate(p0, d[i + 1, pl.ds(1, ny + 2)], i, ny + 2)
            r[i + 1, pl.ds(1, ny + 2)] = residual
            p1[i] = ahead * p0[i + 1, pl.ds(1, ny + 2)] + along * residual

        rows(nx + 2, second)
        again, around = steps[1]

        def third(i):
            residual = r[i + 2, pl.ds(2, ny)] - operate(p1, d[i + 2, pl.ds(2, ny)], i, ny)
            direction = p1[i + 1, pl.ds(1, ny)]
            last = again * direction + around * residual
            result = u[i + 3, pl.ds(3, ny)] + p0[i + 2, pl.ds(2, ny)] + direction + last
            o[i] = result
            if level:
                C[level - 1][i + 1, pl.ds(1, ny)] = result.astype(jnp.bfloat16)

        rows(nx, third)
        return fetch(o, outs[level])

    def prolong(level):
        nx, ny = dims[level]
        cx, cy = dims[level + 1]
        full = (cx * peers[0], cy * peers[1])
        lift_x = full[0] + 1 - gz * cx
        lift_y = full[1] + 1 - gy * cy

        def pick(i, j, k):
            link = links[level][i, j, k]
            row = modulo(quotient(link, full[1]) + lift_x, full[0])
            col = modulo(modulo(link, full[1]) + lift_y, full[1])
            return C[level][jnp.minimum(row, cx + 1), jnp.minimum(col, cy + 1)]

        def body(i):
            for j in range(ny):
                picked = jnp.concatenate([pick(i, j, 0), pick(i, j, 1)], axis=1)
                block = jnp.concatenate([B[level][i, j, 0], B[level][i, j, 1]], axis=1)
                sums = lax.dot_general(
                    picked, block, (((1,), (1,)), ((), ())), preferred_element_type=jnp.float32
                )
                U[level][i + REACH, j + REACH] = U[level][i + REACH, j + REACH] + sums

        rows(nx, body)

    ready = exchange(U[3], 3, REACH)
    sides = [None] * LEVELS
    for level in reversed(range(LEVELS)):
        sides[level] = exchange(S[level], level, REACH - 1) + exchange(D[level], level, REACH - 1)
    stores = []
    for level in reversed(range(LEVELS)):
        if level < LEVELS - 1:
            block_loads[level].wait()
            prolong(level)
            ready = exchange(U[level], level, REACH)
        for copy in ready + sides[level]:
            copy.wait_recv()
        stores.append(smooth(level))
        if level:
            for copy in exchange(C[level - 1], level, 1, True):
                copy.wait_recv()
    for copy in pending:
        copy.wait_send()
    for copy in stores:
        copy.wait()


def shards(peers, *args):
    dims = [x.shape[:2] for x in args[:4]]
    line = args[0].shape[2:]
    width = line[1:]

    def level_scratch(extra, shape):
        return [pltpu.VMEM((nx + extra, ny + extra) + shape, jnp.float32) for nx, ny in dims]

    scratch = (
        level_scratch(2 * REACH, line)
        + level_scratch(2 * REACH - 2, line)
        + level_scratch(2 * REACH - 2, (1,) + width)
        + level_scratch(2 * REACH - 2, line)
        + level_scratch(2 * REACH - 2, line)
        + level_scratch(2 * REACH - 4, line)
        + level_scratch(0, line)
        + [pltpu.VMEM(x.shape, x.dtype) for x in args[12:15]]
        + [pltpu.VMEM((nx + 2, ny + 2) + line, jnp.bfloat16) for nx, ny in dims[1:]]
        + level_scratch(0, width)
    )
    messages = message_count(dims)
    scratch += [
        pltpu.SemaphoreType.DMA((24,)),
        pltpu.SemaphoreType.DMA((messages,)),
        pltpu.SemaphoreType.DMA((messages,)),
    ]
    anywhere = pl.BlockSpec(memory_space=pl.ANY)
    outs = pl.pallas_call(
        partial(kernel, dims, peers),
        out_shape=[jax.ShapeDtypeStruct(x.shape, x.dtype) for x in args[:4]],
        in_specs=[anywhere] * 15 + [pl.BlockSpec(memory_space=pltpu.SMEM)] * 3,
        out_specs=[anywhere] * 4,
        scratch_shapes=scratch,
        compiler_params=pltpu.CompilerParams(
            collective_id=0, has_side_effects=True, vmem_limit_bytes=40 * 1024 * 1024
        ),
    )(*args)
    return tuple(outs)


def solution(mesh):
    peers = (mesh.shape["gz"], mesh.shape["gy"])
    grid = P("gz", "gy")
    return jax.shard_map(
        partial(shards, peers),
        mesh=mesh,
        in_specs=(grid,) * 18,
        out_specs=(grid,) * 4,
        check_vma=False,
    )
```

time: 166 us -> 93.6 us (0.56)
  Pallas kernels: 0 us -> 73.2 us
  starting transfers between devices: 70.2 us -> 0 us
  waiting for transfers between devices: 60.8 us -> 0 us
  blocking collectives: 12.5 us -> 0 us
  local copies, waits for them, and re-layouts: 6.72 us -> 18.9 us
  other arithmetic: 9.63 us -> 0 us
  matrix products: 4.93 us -> 0 us
    pallas_call x0 -> x1, Pallas kernels: none -> 73.2 us  [shards(): pl.pallas_call(partial(kernel, dims, peers), out_shape=[jax.ShapeDtypeStr...]
    ppermute x44 -> x0, starting transfers between devices: 70.2 us -> none  [the longest x22 59.3 us: padded(): after = lax.ppermute(initial, axis, down)]
    ppermute x44 -> x0, waiting for transfers between devices: 60.8 us -> none  [the longest x22 43.3 us: padded(): before = lax.ppermute(last, axis, up)]
    unnamed x10 -> x38, local copies, waits for them, and re-layouts: 0.03 us -> 18.9 us
    all_gather x2 -> x0, blocking collectives: 12.5 us -> none  [gathered_smooth(): lax.all_gather(pack_level(source, initial, diagonal), 'gy', axis=1, tiled...]
    dot_general x3 -> x0, matrix products: 4.93 us -> none  [prolong_local(): jnp.einsum('abkrj,abkij->abri', picked_lines, blocks, preferred_element_t...]
    slice x49 -> x0, local copies, waits for them, and re-layouts: 3.07 us -> none  [the longest x24 2.85 us: line_sum(): return jnp.roll(vector, 1, 3) + jnp.roll(vector, -1, 3)]
    add x7 -> x0, other arithmetic: 2.25 us -> none  [the longest x1 1.32 us: chebyshev(): result = result + direction]
  transfers between devices with their start and end apart: 44 -> 0, of which waited for: 31 -> 0; matrix products, arithmetic and copies ran while one was open for 5% -> 0% of each run, Pallas kernels for 0% -> 0%
where the time goes in v1:
time: 93.6 us; the launch traced here: 92.8 us
  Pallas kernels  73.2 us (78%)
  local copies, waits for them, and re-layouts  18.9 us (20%)
    pallas_call x1, Pallas kernels, shards(): pl.pallas_call(partial(kernel, dims, peers), out_shape=[jax.ShapeDtypeStr...  73.2 us
    unnamed x38, local copies, waits for them, and re-layouts  18.9 us

profile of v1, /device:TPU:0, one launch (start us, length us, event | category | flops | bytes accessed | tf_op | source)
XLA Modules:
  0.0 92.8 jit_solution(9045550629424377539)
XLA Ops:
  0.6 0.8 copy.23.refs_16_
  1.4 0.8 copy.22.refs_15_
  2.2 0.0 copy-start
  2.2 2.2 %copy-done = bf16[8,8,2,128,128]{4,3,2,1,0:T(8,128)(2,1)S(1)} copy-done((bf16[8,8,2,128,128]{4,3,2,1,0:T(8,128)(2,1)S(1)}, bf16[8,8,2,128,128]{4,3,2,1,0:T(8,128)(2,1)}, u32[]{:S(2)}) %copy-start) | copy-done | bytes 4194328
  4.4 0.0 copy-start.1
  4.4 1.2 %copy-done.1 = bf16[4,4,2,128,128]{4,3,2,1,0:T(8,128)(2,1)S(1)} copy-done((bf16[4,4,2,128,128]{4,3,2,1,0:T(8,128)(2,1)S(1)}, bf16[4,4,2,128,128]{4,3,2,1,0:T(8,128)(2,1)}, u32[]{:S(2)}) %copy-start.1) | copy-done | bytes 1048600
  5.6 0.0 copy-start.2
  5.6 1.0 %copy-done.2 = f32[8,8,16,128]{3,2,1,0:T(8,128)S(1)} copy-done((f32[8,8,16,128]{3,2,1,0:T(8,128)S(1)}, f32[8,8,16,128]{3,2,1,0:T(8,128)}, u32[]{:S(2)}) %copy-start.2) | copy-done | bytes 524312
  6.7 0.0 copy-start.3
  6.7 1.0 %copy-done.3 = f32[8,8,16,128]{3,2,1,0:T(8,128)S(1)} copy-done((f32[8,8,16,128]{3,2,1,0:T(8,128)S(1)}, f32[8,8,16,128]{3,2,1,0:T(8,128)}, u32[]{:S(2)}) %copy-start.3) | copy-done | bytes 524312
  7.7 0.0 copy-start.4
  7.7 0.9 %copy-done.4 = bf16[2,2,2,128,128]{4,3,2,1,0:T(8,128)(2,1)S(1)} copy-done((bf16[2,2,2,128,128]{4,3,2,1,0:T(8,128)(2,1)S(1)}, bf16[2,2,2,128,128]{4,3,2,1,0:T(8,128)(2,1)}, u32[]{:S(2)}) %copy-start.4) | copy-done | bytes 262168
  8.7 0.0 copy-start.5
  8.7 0.9 copy-done.5
  9.6 0.0 copy-start.6
  9.6 0.9 copy-done.6
  10.5 0.0 copy-start.7
  10.5 0.8 copy-done.7
  11.2 0.0 copy-start.8
  11.3 0.8 copy-done.8
  12.0 0.0 copy-start.9
  12.0 0.8 copy-done.9
  12.8 0.0 copy-start.10
  12.8 0.7 copy-done.10
  13.5 0.0 copy-start.11
  13.5 0.7 copy-done.11
  14.2 0.0 copy-start.12
  14.2 0.7 copy-done.12
  14.9 0.0 copy-start.13
  14.9 0.7 copy-done.13
  15.5 0.0 copy-start.14
  15.5 0.7 copy-done.14
  16.2 0.0 copy-start.15
  16.2 0.7 copy-done.15
  16.9 73.2 %shard_map.201 = (f32[8,8,16,128]{3,2,1,0:T(8,128)S(1)}, f32[4,4,16,128]{3,2,1,0:T(8,128)S(1)}, f32[2,2,16,128]{3,2,1,0:T(8,128)S(1)}, f32[1,1,16,128]{3,2,1,0:T(8,128)S(1)}) custom-call(f32[8,8,16,128]{3,2,1,0:T(8,128)S(1)} %copy-done.2, f32[4,4,16,128]{3,2,1,0:T(8,128)S(1)} %copy-done.5, f32[2,2,16,128]{3,2,1,0:T(8,128)S(1)} %copy-done.7, ...), custom_call_target="tpu_custom_call" | custom-call | tf_op jit(solution)/shard_map/pallas_call | solution.py:287
  90.1 0.8 copy.28
  90.9 0.7 copy.29
  91.5 0.6 copy.30
  92.2 0.6 copy.31
Async XLA Ops:
  2.2 2.2 %copy-start = (bf16[8,8,2,128,128]{4,3,2,1,0:T(8,128)(2,1)S(1)}, bf16[8,8,2,128,128]{4,3,2,1,0:T(8,128)(2,1)}, u32[]{:S(2)}) copy-start(bf16[8,8,2,128,128]{4,3,2,1,0:T(8,128)(2,1)} %refs_12_.1) | copy-start | bytes 12582916
  4.4 1.2 %copy-start.1 = (bf16[4,4,2,128,128]{4,3,2,1,0:T(8,128)(2,1)S(1)}, bf16[4,4,2,128,128]{4,3,2,1,0:T(8,128)(2,1)}, u32[]{:S(2)}) copy-start(bf16[4,4,2,128,128]{4,3,2,1,0:T(8,128)(2,1)} %refs_13_.1) | copy-start | bytes 3145732
  5.6 1.0 %copy-start.2 = (f32[8,8,16,128]{3,2,1,0:T(8,128)S(1)}, f32[8,8,16,128]{3,2,1,0:T(8,128)}, u32[]{:S(2)}) copy-start(f32[8,8,16,128]{3,2,1,0:T(8,128)} %refs_0_.1) | copy-start | bytes 1572868
  6.7 1.0 %copy-start.3 = (f32[8,8,16,128]{3,2,1,0:T(8,128)S(1)}, f32[8,8,16,128]{3,2,1,0:T(8,128)}, u32[]{:S(2)}) copy-start(f32[8,8,16,128]{3,2,1,0:T(8,128)} %refs_4_.1) | copy-start | bytes 1572868
  7.7 0.9 %copy-start.4 = (bf16[2,2,2,128,128]{4,3,2,1,0:T(8,128)(2,1)S(1)}, bf16[2,2,2,128,128]{4,3,2,1,0:T(8,128)(2,1)}, u32[]{:S(2)}) copy-start(bf16[2,2,2,128,128]{4,3,2,1,0:T(8,128)(2,1)} %refs_14_.1) | copy-start | bytes 786436
  8.7 0.9 copy-start.5
  9.6 0.9 copy-start.6
  10.5 0.8 copy-start.7
  11.2 0.8 copy-start.8
  12.0 0.8 copy-start.9
  12.8 0.7 copy-start.10
  13.5 0.7 copy-start.11
  14.2 0.7 copy-start.12
  14.9 0.7 copy-start.13
  15.5 0.7 copy-start.14
  16.2 0.7 copy-start.15

commit v2 on v1

--- a/solution.py
+++ b/solution.py
@@ -237,7 +237,7 @@
 
     ready = exchange(U[3], 3, REACH)
     sides = [None] * LEVELS
-    for level in reversed(range(LEVELS)):
+    for level in reversed(range(1, LEVELS)):
         sides[level] = exchange(S[level], level, REACH - 1) + exchange(D[level], level, REACH - 1)
     stores = []
     for level in reversed(range(LEVELS)):
@@ -247,6 +247,8 @@
             ready = exchange(U[level], level, REACH)
         for copy in ready + sides[level]:
             copy.wait_recv()
+        if level == 2:
+            sides[0] = exchange(S[0], 0, REACH - 1) + exchange(D[0], 0, REACH - 1)
         stores.append(smooth(level))
         if level:
             for copy in exchange(C[level - 1], level, 1, True):
@@ -291,7 +293,7 @@
         out_specs=[anywhere] * 4,
         scratch_shapes=scratch,
         compiler_params=pltpu.CompilerParams(
-            collective_id=0, has_side_effects=True, vmem_limit_bytes=40 * 1024 * 1024
+            collective_id=0, has_side_effects=True, vmem_limit_bytes=67043328
         ),
     )(*args)
     return tuple(outs)

time: 93.6 us -> 82.6 us (0.88)
  local copies, waits for them, and re-layouts: 18.9 us -> 8.91 us
    unnamed x38 -> x6, local copies, waits for them, and re-layouts: 18.9 us -> 8.91 us
where the time goes in v2:
time: 82.6 us; the launch traced here: 82.1 us
  Pallas kernels  72.6 us (88%)
  local copies, waits for them, and re-layouts  8.91 us (11%)
    pallas_call x1, Pallas kernels, shards(): pl.pallas_call(partial(kernel, dims, peers), out_shape=[jax.ShapeDtypeStr...  72.6 us
    unnamed x6, local copies, waits for them, and re-layouts  8.91 us

profile of v2, /device:TPU:0, one launch (start us, length us, event | category | flops | bytes accessed | tf_op | source)
XLA Modules:
  0.0 82.1 jit_solution(6544067177829204933)
XLA Ops:
  0.6 1.4 %copy.23.refs_16_ = s32[4,4,2]{2,1,0:T(4,128)} copy(s32[4,4,2]{1,2,0:T(2,128)} %param.34) | data formatting | bytes 256 | tf_op args[16]
  2.0 1.4 %copy.22.refs_15_ = s32[8,8,2]{2,1,0:T(8,128)} copy(s32[8,8,2]{1,2,0:T(2,128)} %param.33) | data formatting | bytes 1024 | tf_op args[15]
  3.4 72.6 %shard_map.201 = (f32[8,8,16,128]{3,2,1,0:T(8,128)}, f32[4,4,16,128]{3,2,1,0:T(8,128)}, f32[2,2,16,128]{3,2,1,0:T(8,128)}, f32[1,1,16,128]{3,2,1,0:T(8,128)}) custom-call(f32[8,8,16,128]{3,2,1,0:T(8,128)} %refs_0_.1, f32[4,4,16,128]{3,2,1,0:T(8,128)} %refs_1_.1, f32[2,2,16,128]{3,2,1,0:T(8,128)} %refs_2_.1, f32[1,1,16,128]{3,2,1,0:T(8,128)} %refs_3_.1, ...), custom_call_target="tpu_custom_call" | custom-call | tf_op jit(solution)/shard_map/pallas_call | solution.py:289
  76.0 1.9 %copy.28 = f32[8,8,16,128]{3,2,1,0:T(8,128)} copy(f32[8,8,16,128]{3,2,1,0:T(8,128)} %get-tuple-element.8) | data formatting | bytes 1048576
  77.9 1.6 %copy.29 = f32[4,4,16,128]{3,2,1,0:T(8,128)} copy(f32[4,4,16,128]{3,2,1,0:T(8,128)} %get-tuple-element.9) | data formatting | bytes 262144
  79.5 1.4 %copy.30 = f32[2,2,16,128]{3,2,1,0:T(8,128)} copy(f32[2,2,16,128]{3,2,1,0:T(8,128)} %get-tuple-element.10) | data formatting | bytes 65536
  80.8 1.3 %copy.31 = f32[1,1,16,128]{3,2,1,0:T(8,128)} copy(f32[1,1,16,128]{3,2,1,0:T(8,128)} %get-tuple-element.11) | data formatting | bytes 16384
